TPU v7x, 32 devices: a whole 2x2x4 slice. The times are simulated.
32 devices in a mesh: gx: 8 (over y, x, core), gy: 4 (over z).
Axes of the slice: x: 2, y: 2, z: 4, core: 2. Of those that a mesh axis runs over, the one named last changes fastest.
Arguments:
- layer_early: bfloat16 [1024, 8192], P(None, ('gx', 'gy')), may hold values from -48 to 48
- layer_late: bfloat16 [1024, 8192], P(('gx', 'gy')), may hold values from -48 to 48
Outputs:
- similarity: float32 [], replicated
- token_share: float32 [1024], P(('gx', 'gy'))
- early_rows: bfloat16 [1024, 8192], P(('gx', 'gy'))
- late_rows: bfloat16 [1024, 8192], P(('gx', 'gy'))
All inputs are finite; a program needn't handle non-finite values.
Results may differ from a plain program's by a relative error of at most 0.0015.
Values may be sent and summed in bfloat16 or wider, within the bound.
A program may use at most 128 MiB of HBM per device.

v0:
```python
import jax
import jax.numpy as jnp
from jax import lax
from jax.sharding import PartitionSpec as P


def pair_terms(left_early, left_late, right_early, right_late):
    dims = (((1,), (1,)), ((), ()))
    block_early = lax.dot_general(left_early, right_early, dims, preferred_element_type=jnp.float32)
    block_late = lax.dot_general(left_late, right_late, dims, preferred_element_type=jnp.float32)
    return (
        jnp.sum(block_early * block_late, axis=1),
        jnp.sum(block_early * block_early),
        jnp.sum(block_late * block_late),
    )


def body(layer_early, layer_late):
    total_rows = layer_early.shape[0]
    early_values = layer_early.astype(jnp.float32)
    early_cols = (early_values - jnp.mean(early_values, axis=0)).astype(jnp.bfloat16)
    late_values = layer_late.astype(jnp.float32)
    column_sums = lax.psum(jnp.sum(late_values, axis=0), ("gx", "gy"))
    late_rows = (late_values - column_sums / total_rows).astype(jnp.bfloat16)
    early_rows = lax.all_to_all(early_cols, ("gx", "gy"), split_axis=0, concat_axis=1, tiled=True)
    block_early, block_late = (
        lax.all_gather(early_rows, "gy", axis=0, tiled=True),
        lax.all_gather(late_rows, "gy", axis=0, tiled=True),
    )
    row_part, early_part, late_part = pair_terms(
        block_early,
        block_late,
        lax.all_gather(early_rows, "gx", axis=0, tiled=True),
        lax.all_gather(late_rows, "gx", axis=0, tiled=True),
    )
    own_align = lax.psum_scatter(row_part, "gy", scatter_dimension=0, tiled=True)
    total_kl, total_kk, total_ll = lax.psum(
        (jnp.sum(row_part), early_part, late_part), ("gx", "gy")
    )
    scale_norm = jnp.sqrt(total_kk * total_ll)
    similarity = total_kl / scale_norm
    token_share = total_rows * own_align / scale_norm
    return (similarity, token_share, early_rows, late_rows)


def solution(mesh):
    in_specs = (P(None, ("gx", "gy")), P(("gx", "gy"), None))
    out_specs = (P(), P(("gx", "gy")), P(("gx", "gy"), None), P(("gx", "gy"), None))
    return jax.shard_map(body, mesh=mesh, in_specs=in_specs, out_specs=out_specs, check_vma=False)
```

profile of v0, /device:TPU:0, one launch (start us, length us, event | category | flops | bytes accessed | tf_op | source)
XLA Modules:
  0.0 298.2 jit_solution(8457581897998979989)
XLA Ops:
  7.2 0.0 all-gather.9.cloned.1.call-start
  7.2 1.2 convert_reduce_fusion
  8.4 42.1 %psum.28 = f32[8192]{0:T(1024)S(1)} all-reduce(f32[8192]{0:T(1024)S(1)} %convert_reduce_fusion), channel_id=1, replica_groups=mesh['gx'=8,'gy'=4] {'gx','gy'}, use_global_device_ids=true, to_apply=%region_2.0 | all-reduce | flops 8192 | bytes 65536 | tf_op jit(solution)/shard_map/psum | solution.py:23
  50.6 1.9 fusion.1
  52.5 0.0 all-gather.11.cloned.1.call-start
  52.5 0.7 all-gather.11.cloned.1.call-update
  53.3 0.0 all-gather.5.cloned.1.call-start
  53.3 1.2 convert_reduce_fusion.1
  54.5 1.1 fusion
  55.6 28.2 %all_to_all.19 = bf16[32,32,256]{2,1,0:T(8,128)(2,1)S(1)} all-to-all(bf16[32,32,256]{2,1,0:T(8,128)(2,1)S(1)} %bitcast.12), channel_id=1, replica_groups=mesh['gx'=8,'gy'=4] {'gx','gy'}, dimensions={0} | all-to-all | bytes 1048576 | tf_op jit(solution)/shard_map/all_to_all | solution.py:25
  83.9 0.8 copy.8
  84.7 0.0 all-gather.5.cloned.1.call-update
  84.7 0.0 all-gather.7.cloned.1.call-start
  84.8 0.5 all-gather.7.cloned.1.call-update
  85.3 0.6 dynamic-slice
  86.6 22.4 %all-gather.9.cloned.1.call-done = bf16[128,8192]{1,0:T(8,128)(2,1)} async-done(((bf16[32,8192]{1,0:T(8,128)(2,1)}), bf16[128,8192]{1,0:T(8,128)(2,1)}) %all-gather.9.cloned.1.call-update) | async-done | bytes 2097168 | tf_op jit(solution)/shard_map/all_gather | solution.py:28
  109.0 38.1 %all-gather.11.cloned.1.call-done = bf16[256,8192]{1,0:T(8,128)(2,1)} async-done(((bf16[32,8192]{1,0:T(8,128)(2,1)}), bf16[256,8192]{1,0:T(8,128)(2,1)}) %all-gather.11.cloned.1.call-update) | async-done | bytes 4194320 | tf_op jit(solution)/shard_map/all_gather | solution.py:34
  147.1 4.4 %fusion.3 = f32[128,256]{1,0:T(8,128)S(1)} fusion(bf16[128,8192]{1,0:T(8,128)(2,1)} %all-gather.9.cloned.1.call-done, bf16[256,8192]{1,0:T(8,128)(2,1)} %all-gather.11.cloned.1.call-done), kind=kOutput, calls=%fused_computation.14 | convolution fusion | flops 536870912 | bytes 6422528 | tf_op jit(solution)/shard_map/dot_general | solution.py:10
  151.5 43.5 %all-gather.5.cloned.1.call-done = bf16[128,8192]{1,0:T(8,128)(2,1)} async-done(((bf16[32,8192]{1,0:T(8,128)(2,1)}), bf16[128,8192]{1,0:T(8,128)(2,1)}) %all-gather.5.cloned.1.call-update) | async-done | bytes 2097168 | tf_op jit(solution)/shard_map/all_gather | solution.py:27
  195.0 37.7 %all-gather.7.cloned.1.call-done = bf16[256,8192]{1,0:T(8,128)(2,1)} async-done(((bf16[32,8192]{1,0:T(8,128)(2,1)}), bf16[256,8192]{1,0:T(8,128)(2,1)}) %all-gather.7.cloned.1.call-update) | async-done | bytes 4194320 | tf_op jit(solution)/shard_map/all_gather | solution.py:33
  232.7 5.0 %multiply_reduce_fusion.2 = (f32[128]{0:T(128)S(1)}, f32[]{:T(128)}, f32[]{:T(128)}, f32[]{:T(128)}) fusion(f32[128,256]{1,0:T(8,128)S(1)} %fusion.3, bf16[128,8192]{1,0:T(8,128)(2,1)} %all-gather.5.cloned.1.call-done, bf16[256,8192]{1,0:T(8,128)(2,1)} %all-gather.7.cloned.1.call-done), kind=kOutput, calls=%fused_computation.8 | convolution fusion | flops 537100160 | bytes 6423052 | tf_op jit(solution)/shard_map/dot_general | solution.py:9
  237.7 39.6 %all-reduce.1 = (f32[]{:T(128)}, f32[]{:T(128)}, f32[]{:T(128)}) all-reduce(f32[]{:T(128)} %get-tuple-element.5, f32[]{:T(128)} %get-tuple-element.7, f32[]{:T(128)} %get-tuple-element.6), channel_id=1, replica_groups=mesh['gx'=8,'gy'=4] {'gx','gy'}, use_global_device_ids=true, to_apply=%region_4.0 | all-reduce | flops 3 | bytes 24 | tf_op jit(solution)/shard_map/psum | solution.py:37
  278.7 10.6 %all-reduce = f32[128]{0:T(128)S(1)} all-reduce(f32[128]{0:T(128)S(1)} %get-tuple-element.4), channel_id=2, replica_groups=mesh['gx'=8,'gy'=4] {'gy'}, use_global_device_ids=true, to_apply=%region_10.0.clone | all-reduce | flops 128 | bytes 1024
  290.0 0.6 fusion.2
  (5 shorter events, 0.0 us)
Async XLA Ops:
  7.2 78.2 %copy-start = (u32[32]{0:T(128)S(1)}, u32[32]{0:T(128)}, u32[]{:S(2)}) copy-start(u32[32]{0:T(128)} %constant.11) | copy-start | bytes 388
  7.2 101.8 %all-gather.9.cloned.1.call-start = ((), (), s32[]{:S(2)}) async-start(), calls=%async_computation.3 | async-start | bytes 2621440 | tf_op jit(solution)/shard_map/all_gather | solution.py:28
  52.5 94.6 %all-gather.11.cloned.1.call-start = ((), (), s32[]{:S(2)}) async-start(), calls=%async_computation.4 | async-start | bytes 4718592 | tf_op jit(solution)/shard_map/all_gather | solution.py:34
  53.3 141.7 %all-gather.5.cloned.1.call-start = ((), (), s32[]{:S(2)}) async-start(), calls=%async_computation.1 | async-start | bytes 2621440 | tf_op jit(solution)/shard_map/all_gather | solution.py:27
  84.7 147.9 %all-gather.7.cloned.1.call-start = ((), (), s32[]{:S(2)}) async-start(), calls=%async_computation.2 | async-start | bytes 4718592 | tf_op jit(solution)/shard_map/all_gather | solution.py:33
Sparse Core Ops, SparseCore 0:
  52.6 56.3 all-gather.8
  111.5 35.5 all-gather.10
  149.3 45.6 all-gather.4
  197.3 35.3 all-gather.6
where the time goes:
time: 299 us; the launch traced here: 298 us
  waiting for transfers between devices  143 us (48%)
  blocking collectives  121 us (40%)
  between operations  17.6 us (6%)
  matrix products  9.4 us (3%)
  other arithmetic  6.03 us (2%)
    all_gather x1, waiting for transfers between devices, body(): lax.all_gather(early_rows, 'gy', axis=0, tiled=True)  43.5 us
    psum x1, blocking collectives, body(): column_sums = lax.psum(jnp.sum(late_values, axis=0), ('gx', 'gy'))  42.1 us
    psum x1, blocking collectives, body(): lax.psum((jnp.sum(row_part), early_part, late_part), ('gx', 'gy'))  39.6 us
    all_gather x1, waiting for transfers between devices, body(): lax.all_gather(late_rows, 'gx', axis=0, tiled=True)  38.1 us
    all_gather x1, waiting for transfers between devices, body(): lax.all_gather(early_rows, 'gx', axis=0, tiled=True)  37.7 us
    all_to_all x1, blocking collectives, body(): lax.all_to_all(early_cols, ('gx', 'gy'), split_axis=0, concat_axis=1, til...  28.2 us
    all_gather x1, waiting for transfers between devices, body(): lax.all_gather(late_rows, 'gy', axis=0, tiled=True)  22.4 us
    unnamed x1, blocking collectives  10.6 us
  transfers between devices with their start and end apart: 4, of which 4 were waited for; matrix products, arithmetic and copies ran while one was open for 3% of the time, Pallas kernels for 0%

commit v1 on v0

--- a/solution.py
+++ b/solution.py
@@ -20,7 +20,7 @@
     early_values = layer_early.astype(jnp.float32)
     early_cols = (early_values - jnp.mean(early_values, axis=0)).astype(jnp.bfloat16)
     late_values = layer_late.astype(jnp.float32)
-    column_sums = lax.psum(jnp.sum(late_values, axis=0), ("gx", "gy"))
+    column_sums = lax.psum(lax.psum(jnp.sum(late_values, axis=0), "gx"), "gy")
     late_rows = (late_values - column_sums / total_rows).astype(jnp.bfloat16)
     early_rows = lax.all_to_all(early_cols, ("gx", "gy"), split_axis=0, concat_axis=1, tiled=True)
     block_early, block_late = (

time: 299 us -> 298 us (level)
  waiting for transfers between devices: 143 us -> 138 us
  blocking collectives: 121 us -> 125 us
    all_gather x1, waiting for transfers between devices: 22.4 us -> 17.8 us  [body(): lax.all_gather(late_rows, 'gy', axis=0, tiled=True)]
    psum x1 -> x2, blocking collectives: 42.1 us -> 44.8 us  [body(): column_sums = lax.psum(lax.psum(jnp.sum(late_values, axis=0), 'gx'), 'gy')]
where the time goes in v1:
time: 298 us; the launch traced here: 297 us
  waiting for transfers between devices  138 us (46%)
  blocking collectives  125 us (42%)
  between operations  17.6 us (6%)
  matrix products  9.4 us (3%)
  other arithmetic  6.06 us (2%)
    psum x2, blocking collectives, body(): column_sums = lax.psum(lax.psum(jnp.sum(late_values, axis=0), 'gx'), 'gy')  44.8 us
    all_gather x1, waiting for transfers between devices, body(): lax.all_gather(early_rows, 'gy', axis=0, tiled=True)  43.5 us
    psum x1, blocking collectives, body(): lax.psum((jnp.sum(row_part), early_part, late_part), ('gx', 'gy'))  39.6 us
    all_gather x1, waiting for transfers between devices, body(): lax.all_gather(late_rows, 'gx', axis=0, tiled=True)  37.8 us
    all_gather x1, waiting for transfers between devices, body(): lax.all_gather(early_rows, 'gx', axis=0, tiled=True)  37.7 us
    all_to_all x1, blocking collectives, body(): lax.all_to_all(early_cols, ('gx', 'gy'), split_axis=0, concat_axis=1, til...  29.7 us
    all_gather x1, waiting for transfers between devices, body(): lax.all_gather(late_rows, 'gy', axis=0, tiled=True)  17.8 us
    unnamed x1, blocking collectives  10.6 us
  transfers between devices with their start and end apart: 4, of which 4 were waited for; matrix products, arithmetic and copies ran while one was open for 3% of the time, Pallas kernels for 0%

profile of v1, /device:TPU:0, one launch (start us, length us, event | category | flops | bytes accessed | tf_op | source)
XLA Modules:
  0.0 297.4 jit_solution(12857150651782097719)
XLA Ops:
  7.2 0.0 all-gather.9.cloned.1.call-start
  7.2 1.2 convert_reduce_fusion
  8.4 25.5 %psum.35 = f32[8192]{0:T(1024)S(1)} all-reduce(f32[8192]{0:T(1024)S(1)} %convert_reduce_fusion), channel_id=1, replica_groups=mesh['gx'=8,'gy'=4] {'gx'}, use_global_device_ids=true, to_apply=%region_2.0 | all-reduce | flops 8192 | bytes 65536 | tf_op jit(solution)/shard_map/psum | solution.py:23
  33.9 19.2 %psum.36 = f32[8192]{0:T(1024)S(1)} all-reduce(f32[8192]{0:T(1024)S(1)} %psum.35), channel_id=1, replica_groups=mesh['gx'=8,'gy'=4] {'gy'}, use_global_device_ids=true, to_apply=%region_3.0 | all-reduce | flops 8192 | bytes 65536 | tf_op jit(solution)/shard_map/psum | solution.py:23
  53.2 1.9 fusion.1
  55.2 0.0 all-gather.11.cloned.1.call-start
  55.2 0.7 all-gather.11.cloned.1.call-update
  55.9 0.0 all-gather.5.cloned.1.call-start
  56.0 1.2 convert_reduce_fusion.1
  57.2 1.2 fusion
  58.3 29.7 %all_to_all.19 = bf16[32,32,256]{2,1,0:T(8,128)(2,1)S(1)} all-to-all(bf16[32,32,256]{2,1,0:T(8,128)(2,1)S(1)} %bitcast.12), channel_id=1, replica_groups=mesh['gx'=8,'gy'=4] {'gx','gy'}, dimensions={0} | all-to-all | bytes 1048576 | tf_op jit(solution)/shard_map/all_to_all | solution.py:25
  88.1 0.8 copy.8
  88.9 0.0 all-gather.7.cloned.1.call-start
  89.0 0.5 all-gather.7.cloned.1.call-update
  89.5 0.6 dynamic-slice
  90.8 17.8 %all-gather.9.cloned.1.call-done = bf16[128,8192]{1,0:T(8,128)(2,1)} async-done(((bf16[32,8192]{1,0:T(8,128)(2,1)}), bf16[128,8192]{1,0:T(8,128)(2,1)}) %all-gather.9.cloned.1.call-update) | async-done | bytes 2097168 | tf_op jit(solution)/shard_map/all_gather | solution.py:28
  108.6 37.8 %all-gather.11.cloned.1.call-done = bf16[256,8192]{1,0:T(8,128)(2,1)} async-done(((bf16[32,8192]{1,0:T(8,128)(2,1)}), bf16[256,8192]{1,0:T(8,128)(2,1)}) %all-gather.11.cloned.1.call-update) | async-done | bytes 4194320 | tf_op jit(solution)/shard_map/all_gather | solution.py:34
  146.3 4.4 %fusion.3 = f32[128,256]{1,0:T(8,128)S(1)} fusion(bf16[128,8192]{1,0:T(8,128)(2,1)} %all-gather.9.cloned.1.call-done, bf16[256,8192]{1,0:T(8,128)(2,1)} %all-gather.11.cloned.1.call-done), kind=kOutput, calls=%fused_computation.14 | convolution fusion | flops 536870912 | bytes 6422528 | tf_op jit(solution)/shard_map/dot_general | solution.py:10
  150.7 43.5 %all-gather.5.cloned.1.call-done = bf16[128,8192]{1,0:T(8,128)(2,1)} async-done(((bf16[32,8192]{1,0:T(8,128)(2,1)}), bf16[128,8192]{1,0:T(8,128)(2,1)}) %all-gather.5.cloned.1.call-update) | async-done | bytes 2097168 | tf_op jit(solution)/shard_map/all_gather | solution.py:27
  194.2 37.7 %all-gather.7.cloned.1.call-done = bf16[256,8192]{1,0:T(8,128)(2,1)} async-done(((bf16[32,8192]{1,0:T(8,128)(2,1)}), bf16[256,8192]{1,0:T(8,128)(2,1)}) %all-gather.7.cloned.1.call-update) | async-done | bytes 4194320 | tf_op jit(solution)/shard_map/all_gather | solution.py:33
  231.9 5.0 %multiply_reduce_fusion.2 = (f32[128]{0:T(128)S(1)}, f32[]{:T(128)}, f32[]{:T(128)}, f32[]{:T(128)}) fusion(f32[128,256]{1,0:T(8,128)S(1)} %fusion.3, bf16[128,8192]{1,0:T(8,128)(2,1)} %all-gather.5.cloned.1.call-done, bf16[256,8192]{1,0:T(8,128)(2,1)} %all-gather.7.cloned.1.call-done), kind=kOutput, calls=%fused_computation.8 | convolution fusion | flops 537100160 | bytes 6423052 | tf_op jit(solution)/shard_map/dot_general | solution.py:9
  236.9 39.6 %all-reduce.1 = (f32[]{:T(128)}, f32[]{:T(128)}, f32[]{:T(128)}) all-reduce(f32[]{:T(128)} %get-tuple-element.5, f32[]{:T(128)} %get-tuple-element.7, f32[]{:T(128)} %get-tuple-element.6), channel_id=1, replica_groups=mesh['gx'=8,'gy'=4] {'gx','gy'}, use_global_device_ids=true, to_apply=%region_5.0 | all-reduce | flops 3 | bytes 24 | tf_op jit(solution)/shard_map/psum | solution.py:37
  277.9 10.6 %all-reduce = f32[128]{0:T(128)S(1)} all-reduce(f32[128]{0:T(128)S(1)} %get-tuple-element.4), channel_id=2, replica_groups=mesh['gx'=8,'gy'=4] {'gy'}, use_global_device_ids=true, to_apply=%region_11.0.clone | all-reduce | flops 128 | bytes 1024
  289.2 0.6 fusion.2
  (6 shorter events, 0.1 us)
Async XLA Ops:
  7.2 82.4 %copy-start = (u32[32]{0:T(128)S(1)}, u32[32]{0:T(128)}, u32[]{:S(2)}) copy-start(u32[32]{0:T(128)} %constant.11) | copy-start | bytes 388
  7.2 101.4 %all-gather.9.cloned.1.call-start = ((), (), s32[]{:S(2)}) async-start(), calls=%async_computation.3 | async-start | bytes 2621440 | tf_op jit(solution)/shard_map/all_gather | solution.py:28
  55.2 91.2 %all-gather.11.cloned.1.call-start = ((), (), s32[]{:S(2)}) async-start(), calls=%async_computation.4 | async-start | bytes 4718592 | tf_op jit(solution)/shard_map/all_gather | solution.py:34
  55.9 138.2 %all-gather.5.cloned.1.call-start = ((), (), s32[]{:S(2)}) async-start(), calls=%async_computation.1 | async-start | bytes 2621440 | tf_op jit(solution)/shard_map/all_gather | solution.py:27
  88.9 143.0 %all-gather.7.cloned.1.call-start = ((), (), s32[]{:S(2)}) async-start(), calls=%async_computation.2 | async-start | bytes 4718592 | tf_op jit(solution)/shard_map/all_gather | solution.py:33
Sparse Core Ops, SparseCore 0:
  55.3 53.2 all-gather.8
  111.0 35.2 all-gather.10
  148.5 45.6 all-gather.4
  196.5 35.3 all-gather.6
